TPU v7x, 32 devices: a whole 2x2x4 slice. The times are simulated.
32 devices in a mesh: col: 4 (over z), row: 8 (over y, x, core).
Axes of the slice: x: 2, y: 2, z: 4, core: 2. Of those that a mesh axis runs over, the one named last changes fastest.
Arguments:
- inter_mask: int32 [4096, 65536], P('row', 'col')
- emb_user: bfloat16 [4096, 32], P(('row', 'col'))
- emb_item: bfloat16 [65536, 32], P(('col', 'row'))
- triples: int32 [4096, 3], replicated
Outputs:
- output 1: bfloat16 [4096, 32], P(('row', 'col'))
- output 2: bfloat16 [65536, 32], P(('col', 'row'))
- output 3: float32 [4096], replicated
All inputs are finite; a program needn't handle non-finite values.
Results may differ from a plain program's by a relative error of at most 0.00855594.
Values are sent between devices in bfloat16 or wider.
A program may use at most 1 GiB of HBM per device.

v0:
```python
import functools

import jax
import jax.numpy as jnp
from jax import lax
from jax.experimental import pallas as pl
from jax.experimental.pallas import tpu as pltpu
from jax.sharding import PartitionSpec as P

LAYERS = 3
ROWS = 8
COLS = 4
SLOTS = 4
CHUNKS = 16
STRIP = 32
EARLY = 6
RELAY0 = 13
GROUP = 256
OFFSET = 256.0
MESH_ID = pl.DeviceIdType.MESH
F32 = jnp.float32
BF16 = jnp.bfloat16

DEG = 0
UDEG = 28
AG = 31
ZAG = AG + 30
ZRS = ZAG + 9
RS_D = ZRS + 9
RS_1 = RS_D + 12
RS_2 = RS_1 + 12
OUZ = RS_2 + 6
OUR = OUZ + 3
MGZ = OUR + 28
MGR = MGZ + 6
N_SEM = MGR + 14


def nt_dot(a, b):
    return lax.dot_general(a, b, (((1,), (1,)), ((), ())), preferred_element_type=F32)


def kernel(mask_hbm, eu_hbm, ei_hbm, ids_hbm, outu_hbm, outi_hbm, loss_hbm,
           a_ref, mbuf, deg_own, deg_out, deg_in, deg_inv, udeg_part, udeg_own, udeg_in, su_ref,
           part, d_in, r1_in, r2_in, eig, eug, pu_acc, pu, pu_in, tot_i, tot_u,
           items_lo, up_rows, down_rows, u_rows, mg, mg_z, mg_zsum, mg_r, ids_ref, outi_ref, hot_ref,
           copy_sem, in_sem, send_sem, recv_sem):
    emb, seg = tot_i.shape
    users, block = a_ref.shape
    ush = tot_u.shape[1]
    cw = block // CHUNKS
    dw = block // 32
    row = lax.axis_index("row")
    col = lax.axis_index("col")
    core = lax.rem(row, 2)
    quad = row // 2
    partner = row + 1 - 2 * core
    at_x, at_y = lax.rem(quad, 2), quad // 2
    half = emb // 2
    sent = []

    def flipped(j):
        fx, fy = (j % 2 if isinstance(j, int) else lax.rem(j, 2)), j // 2
        return (at_y + fy - 2 * at_y * fy) * 2 + at_x + fx - 2 * at_x * fx

    x_row, y_row = 2 * flipped(1) + core, 2 * flipped(2) + core

    def remote(src, dst, idx, **where):
        return pltpu.make_async_remote_copy(
            src_ref=src, dst_ref=dst, send_sem=send_sem.at[idx], recv_sem=recv_sem.at[idx],
            device_id=where, device_id_type=MESH_ID)

    def send(src, dst, idx, **where):
        copy = remote(src, dst, idx, **where)
        copy.start()
        sent.append(copy)

    def arrived(dst, idx):
        remote(dst, dst, idx, row=row).wait_recv()

    def mask_copy(j):
        return pltpu.make_async_copy(
            mask_hbm.at[:, pl.ds(j * cw, cw)], mbuf.at[j % SLOTS], copy_sem.at[j % SLOTS])

    small = [
        pltpu.make_async_copy(eu_hbm, eug.at[0, col], in_sem.at[0]),
        pltpu.make_async_copy(ei_hbm, eig.at[0, row], in_sem.at[1]),
        pltpu.make_async_copy(ids_hbm, ids_ref, in_sem.at[2]),
    ]
    small[0].start()
    small[1].start()
    for j in range(SLOTS):
        mask_copy(j).start()
    small[2].start()

    barrier = pltpu.get_barrier_semaphore()
    for k in range(1, ROWS):
        pl.semaphore_signal(barrier, inc=1, device_id={"row": lax.rem(row + k, ROWS)}, device_id_type=MESH_ID)
    for k in range(1, COLS):
        pl.semaphore_signal(barrier, inc=1, device_id={"col": lax.rem(col + k, COLS)}, device_id_type=MESH_ID)

    lo, hi = pl.ds(0, half), pl.ds(half, half)
    d_row = 2 * flipped(3) + core

    def items_out(layer):
        base = AG + 10 * layer
        low, high = eig.at[layer, row, lo], eig.at[layer, row, hi]
        send(low, low, base, row=x_row)
        send(high, high, base + 1, row=y_row)
        send(high, high, base + 2, row=x_row)
        send(low, low, base + 3, row=y_row)
        send(eig.at[layer, row], eig.at[layer, row], base + 6, row=partner)

    def items_relay(layer):
        base = AG + 10 * layer
        low, high = eig.at[layer, x_row, lo], eig.at[layer, y_row, hi]
        arrived(low, base)
        send(low, low, base + 4, row=y_row)
        arrived(high, base + 1)
        send(high, high, base + 5, row=x_row)

    def items_near(layer):
        base = AG + 10 * layer
        arrived(eig.at[layer, x_row, hi], base + 2)
        send(eig.at[layer, x_row], eig.at[layer, x_row], base + 7, row=partner)
        arrived(eig.at[layer, y_row, lo], base + 3)
        send(eig.at[layer, y_row], eig.at[layer, y_row], base + 8, row=partner)

    def items_far(layer):
        base = AG + 10 * layer
        arrived(eig.at[layer, d_row, lo], base + 4)
        arrived(eig.at[layer, d_row, hi], base + 5)
        remote(eig.at[layer, d_row], eig.at[layer, d_row], base + 9, row=partner).start()

    def items_from_partner(layer, j):
        arrived(eig.at[layer, 2 * flipped(j) + 1 - core], AG + 10 * layer + 6 + j)

    def users_out(layer):
        src = eug.at[layer, col]
        for k in range(1, COLS):
            send(src, src, ZAG + 3 * layer + k - 1, col=lax.rem(col + k, COLS))

    def users_in(layer):
        for k in range(COLS - 1):
            arrived(eug.at[layer, 0], ZAG + 3 * layer + k)

    udeg_part[...] = jnp.zeros_like(udeg_part)
    udeg_own[...] = jnp.zeros_like(udeg_own)
    ready = {max(4 * g + 3, EARLY - 1): (g,) for g in range(4)}
    for j in range(CHUNKS):
        with jax.named_scope("mask_wait"):
            mask_copy(j).wait()

        def strip(s, acc, j=j):
            rows = pl.ds(pl.multiple_of(s * STRIP, STRIP), STRIP)
            m = mbuf[j % SLOTS, rows, :].astype(F32)
            a_ref[rows, j * cw:(j + 1) * cw] = m.astype(BF16)
            lanes = m[:, 0:128]
            for t in range(1, cw // 128):
                lanes = lanes + m[:, t * 128:(t + 1) * 128]
            udeg_part[rows, :] = udeg_part[rows, :] + lanes
            for t in range(STRIP // 8):
                acc = acc + m[t * 8:(t + 1) * 8, :]
            return acc

        acc = lax.fori_loop(0, users // STRIP, strip, jnp.zeros((8, cw), F32))
        if j + SLOTS < CHUNKS:
            mask_copy(j + SLOTS).start()
        total = jnp.sum(acc, axis=0, keepdims=True)
        deg_own[2 * j:2 * j + 1, :] = total[:, :dw]
        deg_own[2 * j + 1:2 * j + 2, :] = total[:, dw:]
        if j == EARLY - 1:
            with jax.named_scope("barrier"):
                pl.semaphore_wait(barrier, ROWS + COLS - 2)
            small[0].wait()
            users_out(0)
            small[1].wait()
            items_out(0)
        if j == RELAY0:
            with jax.named_scope("relay"):
                items_relay(0)
        for g in ready.get(j, ()):
            deg_out[g] = (deg_own[8 * g:8 * g + 8, :] - OFFSET).astype(BF16)
            for k in range(1, ROWS):
                send(deg_out.at[g], deg_in.at[k, g],
                     DEG + 7 * g + k - 1, row=lax.rem(row + k, ROWS))

    counts = nt_dot(jnp.ones((8, 128), BF16), udeg_part[...].astype(BF16))
    for b in range(users // 128):
        udeg_own[b:b + 1, :] = counts[0:1, b * 128:(b + 1) * 128]
    for k in range(1, COLS):
        send(udeg_own, udeg_in.at[k], UDEG + k - 1, col=lax.rem(col + k, COLS))
    tot_u[...] = eug[0, col].astype(F32)
    tot_i[...] = eig[0, row].astype(F32)
    small[2].wait()
    batch = ids_ref.shape[1]
    n_chunks, tw = up_rows.shape[0], up_rows.shape[2]

    def ids_of(which, ch):
        return ids_ref[which:which + 1, pl.ds(pl.multiple_of(ch * tw, 128), tw)]

    def make_hot(ch, carry):
        for which in range(3):
            low_bits = lax.rem(ids_of(which, ch), GROUP)
            same = lax.broadcasted_iota(jnp.int32, (GROUP, tw), 0) == low_bits
            hot_ref[which, ch] = jnp.where(same, 1.0, 0.0).astype(BF16)
        return carry

    with jax.named_scope("make_hot"):
        lax.fori_loop(0, n_chunks, make_hot, 0)
    users_in(0)
    with jax.named_scope("items0"):
        items_near(0)
        items_far(0)
        for k in range(4):
            items_from_partner(0, k)
    with jax.named_scope("udeg_wait"):
        for k in range(1, COLS):
            arrived(udeg_in.at[k], UDEG + k - 1)
    du = udeg_own[...] + udeg_in[1] + udeg_in[2] + udeg_in[3]
    su = lax.rsqrt(jnp.maximum(du, 1.0))
    for b in range(users // 128):
        wide = jnp.broadcast_to(su[b:b + 1, :], (128, 128))
        su_ref[b * 128:(b + 1) * 128, :] = wide.T
    with jax.named_scope("ideg_wait"):
        for g in range(4):
            for k in range(1, ROWS):
                arrived(deg_in.at[k, g], DEG + 7 * g + k - 1)
    for g in range(4):
        di = deg_own[8 * g:8 * g + 8, :] + OFFSET * (ROWS - 1)
        for k in range(1, ROWS):
            di = di + deg_in[k, g].astype(F32)
        deg_inv[8 * g:8 * g + 8, :] = lax.rsqrt(jnp.maximum(di, 1.0))

    def users_all(layer):
        return jnp.concatenate([eug[layer, c] for c in range(COLS)], axis=1)

    def seg_lanes(s, start=0, width=seg):
        return pl.ds(pl.multiple_of(s * seg + start, 128), width)

    def item_dot(layer, s, eu_all):
        for h in range(2):
            part[layer, s, :, h * cw:(h + 1) * cw] = jnp.dot(
                eu_all, a_ref[:, seg_lanes(s, h * cw, cw)], preferred_element_type=F32)

    def d_copy(layer, i, s):
        return remote(part.at[layer, s], d_in.at[layer, i], RS_D + 4 * layer + i, row=partner)

    def x_first(layer, i, s):
        return remote(part.at[layer, s, lo], r1_in.at[layer, i // 2], RS_1 + 4 * layer + i // 2, row=x_row)

    def y_first(layer, i, s):
        return remote(part.at[layer, s, hi], r1_in.at[layer, 2 + i], RS_1 + 4 * layer + 2 + i, row=y_row)

    def plane_start(layer, i, s):
        arrived(d_in.at[layer, i], RS_D + 4 * layer + i)
        part[layer, s] = part[layer, s] + d_in[layer, i]

        @pl.when(jnp.logical_or(i == 0, i == 2))
        def _():
            x_first(layer, i, s).start()

        @pl.when(i < 2)
        def _():
            y_first(layer, i, s).start()

    def item_product(layer, between=None):
        eu_all = users_all(layer)

        def other(i, carry):
            s0, s1 = 2 * flipped(3 - 2 * i) + 1 - core, 2 * flipped(2 - 2 * i) + 1 - core
            item_dot(layer, s0, eu_all)
            item_dot(layer, s1, eu_all)
            d_copy(layer, 2 * i, s0).start()
            d_copy(layer, 2 * i + 1, s1).start()
            return carry

        def own(i, carry):
            s0, s1 = 2 * flipped(3 - 2 * i) + core, 2 * flipped(2 - 2 * i) + core
            item_dot(layer, s0, eu_all)
            item_dot(layer, s1, eu_all)
            plane_start(layer, 2 * i, s0)
            plane_start(layer, 2 * i + 1, s1)
            return carry

        with jax.named_scope("item_other"):
            lax.fori_loop(0, 2, other, 0)
        if between is not None:
            between()
        with jax.named_scope("item_own"):
            lax.fori_loop(0, 2, own, 0)

    def plane_second(layer):
        base = RS_1 + 4 * layer
        arrived(r1_in.at[layer, 0], base)
        part[layer, y_row, lo] = part[layer, y_row, lo] + r1_in[layer, 0]
        send(part.at[layer, y_row, lo], r2_in.at[layer, 0], RS_2 + 2 * layer, row=y_row)
        arrived(r1_in.at[layer, 2], base + 2)
        part[layer, x_row, hi] = part[layer, x_row, hi] + r1_in[layer, 2]
        send(part.at[layer, x_row, hi], r2_in.at[layer, 1], RS_2 + 2 * layer + 1, row=x_row)

    def plane_last(layer):
        base = RS_1 + 4 * layer
        arrived(r1_in.at[layer, 1], base + 1)
        arrived(r1_in.at[layer, 3], base + 3)
        arrived(r2_in.at[layer, 0], RS_2 + 2 * layer)
        arrived(r2_in.at[layer, 1], RS_2 + 2 * layer + 1)
        low = part[layer, row, lo] + r1_in[layer, 1] + r2_in[layer, 0]
        high = part[layer, row, hi] + r1_in[layer, 3] + r2_in[layer, 1]
        cur = jnp.concatenate([low, high], axis=0).astype(BF16)
        if layer + 1 < LAYERS:
            eig[layer + 1, row] = cur
            items_out(layer + 1)
        tot_i[...] = tot_i[...] + cur.astype(F32)

    def user_dots(layer, j):
        s0 = 2 * flipped(j)
        both = nt_dot(a_ref[:, seg_lanes(s0)], eig[layer, s0])
        both = both + nt_dot(a_ref[:, seg_lanes(s0 + 1)], eig[layer, s0 + 1])
        pu_acc[:, 0:emb] = pu_acc[:, 0:emb] + both

    def user_own_chip(layer):
        pu_acc[...] = jnp.zeros_like(pu_acc)
        items_from_partner(layer, 0)
        user_dots(layer, 0)

    def user_chip(layer, j):
        items_from_partner(layer, j)
        user_dots(layer, j)

    def users_reduce_out(layer):
        for c in range(COLS):
            pu[layer, c] = pu_acc[c * ush:(c + 1) * ush, :].T[:emb, :]
        for k in range(1, COLS):
            peer = lax.rem(col + k, COLS)
            send(pu.at[layer, peer], pu_in.at[layer, k], ZRS + 3 * layer + k - 1, col=peer)

    def users_reduce_in(layer):
        for k in range(1, COLS):
            arrived(pu_in.at[layer, k], ZRS + 3 * layer + k - 1)
        total = pu[layer, col] + pu_in[layer, 1] + pu_in[layer, 2] + pu_in[layer, 3]
        cur = total.astype(BF16)
        if layer + 1 < LAYERS:
            eug[layer + 1, col] = cur
            users_out(layer + 1)
        tot_u[...] = tot_u[...] + cur.astype(F32)

    tile = 256
    eu_first = users_all(0)
    n_u = users // tile

    def first_segment(s):
        for h in range(seg // tile):
            cols = seg_lanes(s, h * tile, tile)
            start = h * tile
            inv = deg_inv[pl.ds(s * (seg // dw) + start // dw, 1), start % dw:start % dw + tile]
            items = eig[0, s, :, start:start + tile]
            got = None
            for u in range(n_u):
                rows = slice(u * tile, (u + 1) * tile)
                wide = jnp.concatenate([su_ref[rows, :]] * (tile // 128), axis=1)
                block_a = a_ref[rows, cols] * (wide * inv).astype(BF16)
                a_ref[rows, cols] = block_a
                more = jnp.dot(eu_first[:, rows], block_a, preferred_element_type=F32)
                got = more if got is None else got + more
                pu_acc[rows, 0:emb] = pu_acc[rows, 0:emb] + nt_dot(block_a, items)
            part[0, s, :, start:start + tile] = got

    def first_pair(i, carry):
        theirs, mine = 2 * flipped(3 - i) + 1 - core, 2 * flipped(3 - i) + core
        first_segment(theirs)
        d_copy(0, i, theirs).start()

        @pl.when(i > 0)
        def _():
            plane_start(0, i - 1, 2 * flipped(4 - i) + core)

        first_segment(mine)
        return carry

    pu_acc[...] = jnp.zeros_like(pu_acc)
    with jax.named_scope("first"):
        lax.fori_loop(0, 4, first_pair, 0)
    with jax.named_scope("reduce_out0"):
        users_reduce_out(0)
    with jax.named_scope("second0"):
        plane_start(0, 3, row)
        plane_second(0)
    with jax.named_scope("reduce_in0"):
        users_reduce_in(0)
    with jax.named_scope("last0"):
        plane_last(0)
    with jax.named_scope("users_in1"):
        users_in(1)

    def relay_rows():
        with jax.named_scope("own_chip1"):
            user_own_chip(1)
        with jax.named_scope("relay1"):
            items_relay(1)

    item_product(1, relay_rows)
    with jax.named_scope("near1"):
        items_near(1)
        user_chip(1, 1)
    with jax.named_scope("far1"):
        items_far(1)
    with jax.named_scope("chip1"):
        user_chip(1, 2)
    with jax.named_scope("second1"):
        plane_second(1)
    with jax.named_scope("far_chip1"):
        user_chip(1, 3)
        users_reduce_out(1)
    with jax.named_scope("last1"):
        plane_last(1)
    with jax.named_scope("reduce_in1"):
        users_reduce_in(1)
    with jax.named_scope("own_chip2"):
        user_own_chip(2)
    with jax.named_scope("relay2"):
        items_relay(2)
    with jax.named_scope("users_in2"):
        users_in(2)

    def near_rows():
        with jax.named_scope("near2"):
            items_near(2)

    item_product(2, near_rows)
    with jax.named_scope("far2"):
        items_far(2)
    with jax.named_scope("near_chips2"):
        user_chip(2, 1)
        user_chip(2, 2)
    with jax.named_scope("far_chip2"):
        user_chip(2, 3)
        users_reduce_out(2)
    with jax.named_scope("second2"):
        plane_second(2)
    with jax.named_scope("reduce_in2"):
        users_reduce_in(2)
    scale = 1.0 / (LAYERS + 1)
    u_rows[row, col] = (tot_u[...] * scale).astype(BF16)
    for k in range(1, COLS):
        send(u_rows.at[row, col], u_rows.at[row, col], OUZ + k - 1, col=lax.rem(col + k, COLS))
    def users_over_plane(piece):
        ref = u_rows.at[row, lax.rem(col + COLS - piece, COLS)]
        for k in range(1, ROWS):
            send(ref, ref, OUR + 7 * piece + k - 1, row=lax.rem(row + k, ROWS))

    users_over_plane(0)
    out_copy = [pltpu.make_async_copy(u_rows.at[row, col], outu_hbm, in_sem.at[0])]
    out_copy[0].start()

    def pick(tables, which, ch, first):
        hot = hot_ref[which, ch]
        high_bits = ids_of(which, ch) // GROUP - first
        acc = jnp.zeros((emb, tw), F32)
        for b, table in enumerate(tables):
            got = jnp.dot(table(), hot, preferred_element_type=F32)
            for i in range(4):
                acc = acc + jnp.where(high_bits == b * 4 + i, got[i * emb:(i + 1) * emb, :], 0.0)
        return acc

    with jax.named_scope("plane_last2"):
        plane_last(2)
    out_item = (tot_i[...] * scale).astype(BF16)
    outi_ref[...] = out_item
    out_copy.append(pltpu.make_async_copy(outi_ref, outi_hbm, in_sem.at[1]))
    out_copy[1].start()
    n_lo = seg // GROUP
    for b in range(n_lo):
        items_lo[b] = out_item[:, b * GROUP:(b + 1) * GROUP]
    first = (col * ROWS + row) * n_lo

    with jax.named_scope("ouz_wait"):
        for k in range(1, COLS):
            arrived(u_rows.at[row, 0], OUZ + k - 1)
            users_over_plane(k)

    def pick_items(ch, carry):
        tables = [lambda b=b: items_lo[4 * b:4 * b + 4].reshape(4 * emb, GROUP) for b in range(n_lo // 4)]
        up_rows[ch] = pick(tables, 1, ch, first)
        down_rows[ch] = pick(tables, 2, ch, first)
        return carry

    with jax.named_scope("pick_items"):
        lax.fori_loop(0, n_chunks, pick_items, 0)
    with jax.named_scope("our_wait"):
        for k in range(7 * COLS):
            arrived(u_rows.at[0, 0], OUR + k)

    def user_table(b):
        parts = []
        for i in range(4):
            r, c = (4 * b + i) // 2, 2 * (i % 2)
            parts.append(jnp.concatenate([u_rows[r, c], u_rows[r, c + 1]], axis=1))
        return jnp.concatenate(parts, axis=0)

    def score(pair, carry):
        tables = [lambda b=b: user_table(b) for b in range(ROWS * COLS // 8)]
        for ch in (2 * pair, 2 * pair + 1):
            vec = pick(tables, 0, ch, 0)
            up = jnp.sum(vec * up_rows[ch], axis=0, keepdims=True)
            down = jnp.sum(vec * down_rows[ch], axis=0, keepdims=True)
            diff = up - down
            for t in range(tw // 128):
                mg[pl.ds(ch * (tw // 128) + t, 1), :] = diff[:, t * 128:(t + 1) * 128]
        return carry

    n_rows = mg.shape[0] // 2
    halves = [pl.ds(0, n_rows), pl.ds(n_rows, n_rows)]
    for h, rows in enumerate(halves):
        with jax.named_scope("score"):
            lax.fori_loop(0, n_chunks // 4, lambda p, c, h=h: score(p + h * (n_chunks // 4), c), 0)
        for k in range(1, COLS):
            send(mg.at[rows], mg_z.at[k, rows], MGZ + 3 * h + k - 1, col=lax.rem(col + k, COLS))
    for h, rows in enumerate(halves):
        with jax.named_scope("mgz_wait"):
            for k in range(1, COLS):
                arrived(mg_z.at[k, rows], MGZ + 3 * h + k - 1)
        mg_zsum[rows] = mg[rows] + mg_z[1, rows] + mg_z[2, rows] + mg_z[3, rows]
        for k in range(1, ROWS):
            send(mg_zsum.at[rows], mg_r.at[k, rows], MGR + 7 * h + k - 1, row=lax.rem(row + k, ROWS))
    with jax.named_scope("mgr_wait"):
        for h, rows in enumerate(halves):
            for k in range(1, ROWS):
                arrived(mg_r.at[k, rows], MGR + 7 * h + k - 1)
    margin = mg_zsum[...]
    for k in range(1, ROWS):
        margin = margin + mg_r[k]
    mg_z[0] = jnp.maximum(-margin, 0.0) + jnp.log1p(jnp.exp(-jnp.abs(margin)))
    out_copy.append(pltpu.make_async_copy(mg_z.at[0], loss_hbm, in_sem.at[2]))
    out_copy[2].start()

    for layer in range(LAYERS):
        for i in range(4):
            d_copy(layer, i, row).wait_send()
        for i in range(2):
            x_first(layer, 2 * i, row).wait_send()
            y_first(layer, i, row).wait_send()
        remote(eig.at[layer, row], eig.at[layer, row], AG + 10 * layer + 9, row=partner).wait_send()
    for copy in sent:
        copy.wait_send()
    for copy in out_copy:
        copy.wait()


def write_out(u_ref, i_ref, l_ref, u_out, i_out, l_out):
    u_out[...] = u_ref[...]
    i_out[...] = i_ref[...]
    l_out[...] = l_ref[...]


def solution(mesh):
    def device_body(mask_blk, user_shard, item_shard, triples):
        users, block = mask_blk.shape
        assert users <= 2 * OFFSET and block <= 128 * 256
        emb = user_shard.shape[1]
        ush, seg = user_shard.shape[0], item_shard.shape[0]
        batch = triples.shape[0]
        tw = batch // 8
        dw = block // 32
        hbm = pl.BlockSpec(memory_space=pl.ANY)
        loss_shape = (batch // 128, 128)
        results = (
            jax.ShapeDtypeStruct((emb, ush), BF16),
            jax.ShapeDtypeStruct((emb, seg), BF16),
            jax.ShapeDtypeStruct(loss_shape, F32),
        )
        found = pl.pallas_call(
            kernel,
            out_shape=results,
            in_specs=[pl.BlockSpec(memory_space=pltpu.HBM)] * 4,
            out_specs=(hbm,) * 3,
            scratch_shapes=[
                pltpu.VMEM((users, block), BF16),
                pltpu.VMEM((SLOTS, users, block // CHUNKS), jnp.int32),
                pltpu.VMEM((32, dw), F32),
                pltpu.VMEM((4, 8, dw), BF16),
                pltpu.VMEM((ROWS, 4, 8, dw), BF16),
                pltpu.VMEM((32, dw), F32),
                pltpu.VMEM((users, 128), F32),
                pltpu.VMEM((8, 128), F32),
                pltpu.VMEM((COLS, 8, 128), F32),
                pltpu.VMEM((users, 128), F32),
                pltpu.VMEM((LAYERS, ROWS, emb, seg), F32),
                pltpu.VMEM((LAYERS, 4, emb, seg), F32),
                pltpu.VMEM((LAYERS, 4, emb // 2, seg), F32),
                pltpu.VMEM((LAYERS, 2, emb // 2, seg), F32),
                pltpu.VMEM((LAYERS, ROWS, emb, seg), BF16),
                pltpu.VMEM((LAYERS, COLS, emb, ush), BF16),
                pltpu.VMEM((users, 128), F32),
                pltpu.VMEM((LAYERS, COLS, emb, ush), F32),
                pltpu.VMEM((LAYERS, COLS, emb, ush), F32),
                pltpu.VMEM((emb, seg), F32),
                pltpu.VMEM((emb, ush), F32),
                pltpu.VMEM((seg // GROUP, emb, GROUP), BF16),
                pltpu.VMEM((8, emb, tw), F32),
                pltpu.VMEM((8, emb, tw), F32),
                pltpu.VMEM((ROWS, COLS, emb, ush), BF16),
                pltpu.VMEM(loss_shape, F32),
                pltpu.VMEM((COLS,) + loss_shape, F32),
                pltpu.VMEM(loss_shape, F32),
                pltpu.VMEM((ROWS,) + loss_shape, F32),
                pltpu.VMEM((3, batch), jnp.int32),
                pltpu.VMEM((emb, seg), BF16),
                pltpu.VMEM((3, 8, GROUP, tw), BF16),
                pltpu.SemaphoreType.DMA((SLOTS,)),
                pltpu.SemaphoreType.DMA((3,)),
                pltpu.SemaphoreType.DMA((N_SEM,)),
                pltpu.SemaphoreType.DMA((N_SEM,)),
            ],
            compiler_params=pltpu.CompilerParams(
                collective_id=0, has_side_effects=True, vmem_limit_bytes=56 * 1024 * 1024),
        )(mask_blk, user_shard.T, item_shard.T, triples.T)
        vmem = pl.BlockSpec(memory_space=pltpu.VMEM)
        out_u, out_i, loss = pl.pallas_call(
            write_out, out_shape=results, in_specs=[vmem] * 3, out_specs=(vmem,) * 3,
        )(*found)
        return out_u.T, out_i.T, loss.reshape(batch)

    return jax.shard_map(
        device_body,
        mesh=mesh,
        in_specs=(P("row", "col"), P(("row", "col"), None), P(("col", "row"), None), P()),
        out_specs=(P(("row", "col"), None), P(("col", "row"), None), P()),
        check_vma=False,
    )
```

profile of v0, /device:TPU:0, one launch (start us, length us, event | category | flops | bytes accessed | tf_op | source)
XLA Modules:
  0.0 85.5 jit_solution(11236857677038555520)
XLA Ops:
  0.6 83.3 %shard_map.67 = (bf16[32,128]{1,0:T(8,128)(2,1)}, bf16[32,2048]{1,0:T(8,128)(2,1)}, f32[32,128]{1,0:T(8,128)}) custom-call(s32[512,16384]{1,0:T(8,128)} %mask_hbm.1, bf16[32,128]{1,0:T(8,128)(2,1)} %bitcast.8, bf16[32,2048]{1,0:T(8,128)(2,1)} %bitcast.6, s32[3,4096]{1,0:T(4,128)} %bitcast.7), custom_call_target="tpu_custom_call" | custom-call | tf_op jit(solution)/shard_map/pallas_call | solution.py:572
  83.9 1.6 %shard_map.68 = (bf16[32,128]{1,0:T(8,128)(2,1)}, bf16[32,2048]{1,0:T(8,128)(2,1)}, f32[32,128]{1,0:T(8,128)}) custom-call(bf16[32,128]{1,0:T(8,128)(2,1)} %get-tuple-element.9.u_ref, bf16[32,2048]{1,0:T(8,128)(2,1)} %get-tuple-element.10.i_ref, f32[32,128]{1,0:T(8,128)} %get-tuple-element.11.l_ref), custom_call_target="tpu_custom_call" | custom-call | tf_op jit(solution)/shard_map/pallas_call | solution.py:619
where the time goes:
time: 85.7 us; the launch traced here: 85.5 us
  Pallas kernels  84.9 us (99%)
    pallas_call x1, Pallas kernels, device_body(): pl.pallas_call(kernel, out_shape=results, in_specs=[pl.BlockSpec(memory_s...  83.3 us

commit v1 on v0

--- a/solution.py
+++ b/solution.py
@@ -403,15 +403,15 @@
     with jax.named_scope("near1"):
         items_near(1)
         user_chip(1, 1)
+    with jax.named_scope("chip1"):
+        user_chip(1, 2)
     with jax.named_scope("far1"):
         items_far(1)
-    with jax.named_scope("chip1"):
-        user_chip(1, 2)
-    with jax.named_scope("second1"):
-        plane_second(1)
     with jax.named_scope("far_chip1"):
         user_chip(1, 3)
         users_reduce_out(1)
+    with jax.named_scope("second1"):
+        plane_second(1)
     with jax.named_scope("last1"):
         plane_last(1)
     with jax.named_scope("reduce_in1"):

time: 85.7 us -> 86.1 us (level)
  no operation moved by 1% of the time
where the time goes in v1:
time: 86.1 us; the launch traced here: 85.9 us
  Pallas kernels  85.3 us (99%)
    pallas_call x1, Pallas kernels, device_body(): pl.pallas_call(kernel, out_shape=results, in_specs=[pl.BlockSpec(memory_s...  83.7 us

profile of v1, /device:TPU:0, one launch (start us, length us, event | category | flops | bytes accessed | tf_op | source)
XLA Modules:
  0.0 85.9 jit_solution(1904888985246710866)
XLA Ops:
  0.6 83.7 %shard_map.67 = (bf16[32,128]{1,0:T(8,128)(2,1)}, bf16[32,2048]{1,0:T(8,128)(2,1)}, f32[32,128]{1,0:T(8,128)}) custom-call(s32[512,16384]{1,0:T(8,128)} %mask_hbm.1, bf16[32,128]{1,0:T(8,128)(2,1)} %bitcast.8, bf16[32,2048]{1,0:T(8,128)(2,1)} %bitcast.6, s32[3,4096]{1,0:T(4,128)} %bitcast.7), custom_call_target="tpu_custom_call" | custom-call | tf_op jit(solution)/shard_map/pallas_call | solution.py:572
  84.3 1.6 %shard_map.68 = (bf16[32,128]{1,0:T(8,128)(2,1)}, bf16[32,2048]{1,0:T(8,128)(2,1)}, f32[32,128]{1,0:T(8,128)}) custom-call(bf16[32,128]{1,0:T(8,128)(2,1)} %get-tuple-element.9.u_ref, bf16[32,2048]{1,0:T(8,128)(2,1)} %get-tuple-element.10.i_ref, f32[32,128]{1,0:T(8,128)} %get-tuple-element.11.l_ref), custom_call_target="tpu_custom_call" | custom-call | tf_op jit(solution)/shard_map/pallas_call | solution.py:619
